TPU v7x, 256 devices: a whole 4x4x8 slice. The times are simulated.
256 devices in a mesh: section: 8 (over x, z_lo), dp: 32 (over y, z_hi, core).
Axes of the slice: x: 4, y: 4, z: 8 (z_hi: 4, z_lo: 2; z = z_hi * 2 + z_lo), core: 2. Of those that a mesh axis runs over, the one named last changes fastest.
Arguments:
- activations: bfloat16 [64, 512, 4608], P('section', 'dp'), may hold values from -6 to 6
- section_sources: int32 [64], replicated, may hold values from 0 to 63, as said below
- accumulators: float32 [1024, 16, 4608], P('dp', 'section'), may hold values from -6 to 6
- block_sources: int32 [1024], replicated, may hold values from 0 to 1023, as said below
- loss_terms: float32 [8, 32], P('section', 'dp'), may hold values from 0.35 to 6
- pre_gain: float32 [8, 4608], P('section'), may hold values from 0.1 to 1.9
- query_weight: bfloat16 [8, 4608, 4096], P('section', None, 'dp'), may hold values from -0.09375 to 0.09375
- keyval_weight: bfloat16 [8, 4608, 4096], P('section', None, 'dp'), may hold values from -0.09375 to 0.09375
- output_weight: bfloat16 [8, 4096, 4608], P('section', 'dp'), may hold values from -0.09375 to 0.09375
- post_gain: float32 [8, 4608], P('section'), may hold values from 0.1 to 1.9
Outputs:
- new_activations: bfloat16 [64, 512, 4608], P('section', 'dp')
- new_accumulators: float32 [1024, 16, 4608], P('dp', 'section')
- check_out: bfloat16 [8, 512, 4608], P('section', 'dp')
Inputs may be any that keep to these rules, and one draw needn't show every extreme that they name: `section_sources`: A permutation; each old section's micro-batches fill 1 slots of each new section. `block_sources`: A permutation; each old data index's blocks fill 1 block of each new data index.
All inputs are finite; a program needn't handle non-finite values.
Results may differ from a plain program's by a relative error of at most 0.014.
Values may be sent and summed in bfloat16 or wider, within the bound.
A program may use at most 64 MiB of HBM per device.

v0:
```python
import jax
import jax.numpy as jnp
from jax import lax
from jax.sharding import PartitionSpec as P

D = 4608


def sent_together(arrays, axis, split_dim, concat_dim, along):
    columns = [a.reshape(*a.shape[:along], -1) for a in arrays]
    both = jnp.concatenate(columns, axis=along)
    result, at, finished = (
        lax.all_to_all(both, axis, split_axis=split_dim, concat_axis=concat_dim, tiled=True),
        0,
        [],
    )
    for a, column in zip(arrays, columns):
        piece = result[..., at : at + column.shape[along]]
        finished.append(piece.reshape(*piece.shape[:along], *a.shape[along:]))
        at += column.shape[along]
    return tuple(finished)


def partner(value, axis, stride):
    mask = 2**stride
    pairs = [(source, source ^ mask) for source in range(lax.axis_size(axis))]
    return lax.ppermute(value, axis, pairs)


def rms_norm(values, gain):
    meansq = jnp.mean(values * values, axis=-1, keepdims=True)
    return values * lax.rsqrt(meansq + 1e-06) * gain


def rotary(values, positions):
    width = values.shape[-1]
    middle = width // 2
    counter = jnp.arange(middle, dtype=jnp.float32)
    freqs = 10000.0 ** (-2.0 * counter / width)
    angles = positions.astype(jnp.float32)[:, None] * freqs[None, :]
    cosine = jnp.cos(angles)
    sine = jnp.sin(angles)
    first = values[..., :middle]
    second = values[..., middle:]
    return jnp.concatenate(
        [first * cosine - second * sine, second * cosine + first * sine], axis=-1
    )


def plan_routes(sources, own_index, groups, per_group):
    per_peer = per_group // groups
    table = sources.reshape(groups, per_group)
    owners = table // per_group
    places = table % per_group
    slot_ids = jnp.arange(per_group, dtype=jnp.int32)
    sort_keys = jnp.where(owners == own_index, slot_ids[None, :], slot_ids[None, :] + per_group)
    ranking = jnp.argsort(sort_keys, axis=1)[:, :per_peer]
    send_index = jnp.take_along_axis(places, ranking, axis=1).reshape(-1)
    my_owners = lax.dynamic_slice_in_dim(owners, own_index, 1, 0)[0]
    earlier = (my_owners[None, :] == my_owners[:, None]) & (slot_ids[None, :] < slot_ids[:, None])
    earlier_count = jnp.sum(earlier.astype(jnp.int32), axis=1)
    recv_index = my_owners * per_peer + earlier_count
    return (send_index, recv_index)


def on_device(
    activations,
    section_sources,
    accumulators,
    block_sources,
    loss_terms,
    pre_gain,
    query_weight,
    keyval_weight,
    output_weight,
    post_gain,
):
    sections = lax.axis_size("section")
    section_index = lax.axis_index("section")
    mb_local = activations.shape[0]
    send_index, recv_index = plan_routes(section_sources, section_index, sections, mb_local)
    outgoing = jnp.take(activations, send_index, axis=0)
    incoming = lax.all_to_all(outgoing, "section", split_axis=0, concat_axis=0, tiled=True)
    moved = jnp.take(incoming, recv_index, axis=0)
    data_ranks = lax.axis_size("dp")
    data_index = lax.axis_index("dp")
    blk_local = accumulators.shape[0]
    per_peer = blk_local // data_ranks
    block_send, block_recv = plan_routes(block_sources, data_index, data_ranks, blk_local)
    outgoing_blocks = jnp.take(accumulators, block_send, axis=0)
    term_rows = jnp.broadcast_to(loss_terms, (blk_local, 1))
    incoming_blocks, incoming_terms = tuple(
        (
            part.astype(jnp.float32)
            for part in sent_together(
                (outgoing_blocks.astype(jnp.bfloat16), term_rows.astype(jnp.bfloat16)),
                "dp",
                0,
                0,
                1,
            )
        )
    )
    scale_sum = jnp.sum(incoming_terms[::per_peer, 0])
    factor = data_ranks / scale_sum
    new_accumulators = jnp.take(incoming_blocks, block_recv, axis=0) * factor
    checked = moved[0]
    head_size = query_weight.shape[2]
    is_even = data_index % 2 == 0
    w_query = query_weight[0]
    w_keyval = keyval_weight[0]
    gain_pre = pre_gain[0]
    block_rows = lax.all_gather(checked, "dp", axis=0, tiled=True)
    row_count = block_rows.shape[0]
    positions = jnp.arange(row_count, dtype=jnp.int32)
    normed = rms_norm(block_rows.astype(jnp.float32), gain_pre).astype(jnp.bfloat16)
    queries = jnp.dot(normed, w_query, preferred_element_type=jnp.float32)
    own_proj = jnp.dot(normed, w_keyval, preferred_element_type=jnp.float32)
    queries = rotary(queries, positions)
    own_proj = jnp.where(is_even, rotary(own_proj, positions), own_proj)
    projected = jnp.concatenate([queries, own_proj], axis=1).astype(jnp.bfloat16)
    queries = projected[:, :head_size]
    own_kv = projected[:, head_size:]
    partner_kv = partner(own_kv, "dp", 0)
    key_rows = jnp.where(is_even, own_kv, partner_kv)
    value_rows = jnp.where(is_even, partner_kv, own_kv)
    length = projected.shape[0]
    positions = jnp.arange(length, dtype=jnp.int32)
    scale_factor = (D / data_ranks) ** (-0.5)
    scores = (
        lax.dot_general(
            queries, key_rows, (((1,), (1,)), ((), ())), preferred_element_type=jnp.float32
        )
        * scale_factor
    )
    capped = 50.0 * jnp.tanh(scores / 50.0)
    causal = positions[None, :] <= positions[:, None]
    expd = jnp.where(causal, jnp.exp(capped), 0.0)
    denominator = jnp.sum(expd, axis=-1, keepdims=True)
    probs = expd.astype(jnp.bfloat16)
    numer = jnp.dot(probs, value_rows, preferred_element_type=jnp.float32)
    attended = (numer / denominator).astype(jnp.bfloat16)
    w_output = output_weight[0]
    summed = lax.psum_scatter(
        jnp.dot(attended, w_output, preferred_element_type=jnp.float32).astype(jnp.bfloat16),
        "dp",
        scatter_dimension=0,
        tiled=True,
    ).astype(jnp.float32)
    check_out = (checked.astype(jnp.float32) + rms_norm(summed, post_gain[0])).astype(jnp.bfloat16)
    return (moved, new_accumulators, check_out[None, :, :])


def solution(mesh):
    placed = (
        P("section", "dp", None),
        P(),
        P("dp", "section", None),
        P(),
        P("section", "dp"),
        P("section", None),
        P("section", None, "dp"),
        P("section", None, "dp"),
        P("section", "dp", None),
        P("section", None),
    )
    return jax.shard_map(
        on_device,
        mesh=mesh,
        in_specs=placed,
        out_specs=(P("section", "dp", None), P("dp", "section", None), P("section", "dp", None)),
        check_vma=False,
    )
```

profile of v0, /device:TPU:2, one launch (start us, length us, event | category | flops | bytes accessed | tf_op | source)
XLA Modules:
  0.0 224.1 jit_solution(8892449664727114092)
XLA Ops:
  7.2 0.8 reshape.111
  8.1 0.7 sort.34
  8.8 0.6 gather_fusion
  9.5 1.9 gather_fusion.2
  11.4 1.2 broadcast_select_fusion.1
  12.6 6.2 %all-to-all-start = ((bf16[8,16,4608]{2,1,0:T(8,128)(2,1)}), bf16[8,16,4608]{2,1,0:T(8,128)(2,1)S(1)}, u32[]{:S(2)}, u32[]{:S(2)}) async-start(bf16[8,16,4608]{2,1,0:T(8,128)(2,1)} %broadcast_select_fusion.1), calls=%async_computation | async-start | bytes 2359296 | tf_op jit(solution)/shard_map/all_to_all | solution.py:83
  19.0 14.8 %all-to-all-done = bf16[8,16,4608]{2,1,0:T(8,128)(2,1)S(1)} async-done(((bf16[8,16,4608]{2,1,0:T(8,128)(2,1)}), bf16[8,16,4608]{2,1,0:T(8,128)(2,1)S(1)}, u32[]{:S(2)}, u32[]{:S(2)}) %all-to-all-start) | async-done | bytes 1179680 | tf_op jit(solution)/shard_map/all_to_all | solution.py:83
  33.8 0.6 gather_fusion.3
  34.6 1.0 copy-done.3
  35.6 0.7 slice.56
  36.7 0.8 sort.35
  37.5 0.7 gather_fusion.1
  38.2 61.9 %all-gather.3.cloned.1.call-done = bf16[1,512,4608]{2,1,0:T(8,128)(2,1)} async-done(((bf16[1,16,4608]{2,1,0:T(8,128)(2,1)}), bf16[1,512,4608]{2,1,0:T(8,128)(2,1)}) %all-gather.3.cloned.1.call-update) | async-done | bytes 4718608 | tf_op jit(solution)/shard_map/all_gather | solution.py:113
  100.2 3.5 %fusion = f32[512]{0:T(512)S(1)} fusion(bf16[1,512,4608]{2,1,0:T(8,128)(2,1)} %all-gather.3.cloned.1.call-done), kind=kLoop, calls=%fused_computation.8 | loop fusion | flops 7077376 | bytes 4720640 | tf_op jit(solution)/shard_map/reduce_sum | solution.py:31
  103.9 1.8 fusion.7
  106.9 1.8 fusion.9
  109.7 3.9 %convolution_convert_fusion = bf16[512,4608]{1,0:T(8,128)(2,1)} fusion(bf16[1,128,4608]{2,1,0:T(8,128)(2,1)S(1)} %copy-done, bf16[512,512]{0,1:T(8,128)(2,1)S(1)} %get-tuple-element.28, f32[512]{0:T(512)S(1)} %get-tuple-element.27, bf16[512,128]{0,1:T(8,128)(2,1)S(1)} %collective-permute-done, bf16[512,128]{0,1:T(8,128)(2,1)S(1)} %fusion.21, pred[]{:T(512)S(6)} %eq.57), kind=kOutput, calls=%fused_computation.11 | convolution fusion | flops 673644544 | bytes 6686721 | tf_op jit(solution)/shard_map/dot_general | solution.py:145
  113.7 1.2 copy-done.4
  114.9 1.8 gather_fusion.4
  116.7 0.6 select_convert_fusion
  118.1 2.0 copy.22
  120.1 6.5 %all-to-all-start.1 = ((bf16[32,1,9217]{2,1,0:T(2,128)(2,1)}), bf16[32,1,9217]{2,1,0:T(2,128)(2,1)S(1)}, u32[]{:S(2)}, u32[]{:S(2)}) async-start(bf16[32,1,9217]{2,1,0:T(2,128)(2,1)} %copy.22), calls=%async_computation.1 | async-start | bytes 2392064 | tf_op jit(solution)/shard_map/all_to_all | solution.py:13
  126.6 0.7 reduce.2
  127.5 32.2 %all-to-all-done.1 = bf16[32,1,9217]{2,1,0:T(2,128)(2,1)S(1)} async-done(((bf16[32,1,9217]{2,1,0:T(2,128)(2,1)}), bf16[32,1,9217]{2,1,0:T(2,128)(2,1)S(1)}, u32[]{:S(2)}, u32[]{:S(2)}) %all-to-all-start.1) | async-done | bytes 589920 | tf_op jit(solution)/shard_map/all_to_all | solution.py:13
  159.8 0.8 copy-done.2
  160.7 1.0 reshape.118
  161.7 1.8 gather_fusion.5
  163.5 1.3 convert_reduce_fusion
  165.4 1.6 select_multiply_fusion
  167.1 47.4 %reduce-scatter.2.cloned.1.call-done = bf16[16,4608]{1,0:T(8,128)(2,1)} async-done(((bf16[512,4608]{1,0:T(8,128)(2,1)}), bf16[16,4608]{1,0:T(8,128)(2,1)}) %reduce-scatter.2.cloned.1.call-update) | async-done | bytes 147472 | tf_op jit(solution)/shard_map/reduce_scatter | solution.py:144
  214.4 1.1 fusion.17
  215.5 1.8 fusion.30
  (68 shorter events, 3.7 us)
Async XLA Ops:
  7.2 102.5 %copy-start = (bf16[1,128,4608]{2,1,0:T(8,128)(2,1)S(1)}, bf16[1,128,4608]{2,1,0:T(8,128)(2,1)}, u32[]{:S(2)}) copy-start(bf16[1,128,4608]{2,1,0:T(8,128)(2,1)} %param.22) | copy-start | bytes 3538948
  12.6 21.2 %all-to-all-start = ((bf16[8,16,4608]{2,1,0:T(8,128)(2,1)}), bf16[8,16,4608]{2,1,0:T(8,128)(2,1)S(1)}, u32[]{:S(2)}, u32[]{:S(2)}) async-start(bf16[8,16,4608]{2,1,0:T(8,128)(2,1)} %broadcast_select_fusion.1), calls=%async_computation | async-start | bytes 2359296 | tf_op jit(solution)/shard_map/all_to_all | solution.py:83
  18.7 81.4 %all-gather.3.cloned.1.call-start = ((), (), s32[]{:S(2)}) async-start(), calls=%async_computation.4 | async-start | bytes 4866048 | tf_op jit(solution)/shard_map/all_gather | solution.py:113
  34.4 2.0 copy-start.8
  34.4 2.2 copy-start.6
  34.6 1.0 copy-start.3
  35.6 68.0 %copy-start.9 = (bf16[1,4608,128]{2,1,0:T(8,128)(2,1)S(1)}, bf16[1,4608,128]{2,1,0:T(8,128)(2,1)}, u32[]{:S(2)}) copy-start(bf16[1,4608,128]{2,1,0:T(8,128)(2,1)} %param.21) | copy-start | bytes 3538948
  36.3 178.1 %reduce-scatter.2.cloned.1.call-start = ((), (), s32[]{:S(2)}) async-start(), calls=%async_computation.3 | async-start | bytes 4866048 | tf_op jit(solution)/shard_map/reduce_scatter | solution.py:144
  100.2 3.8 %copy-start.1 = (bf16[1,512,4608]{2,1,0:T(8,128)(2,1)S(1)}, bf16[1,512,4608]{2,1,0:T(8,128)(2,1)}, u32[]{:S(2)}) copy-start(bf16[1,512,4608]{2,1,0:T(8,128)(2,1)} %all-gather.3.cloned.1.call-done) | copy-start | bytes 14155780
  103.9 2.9 %copy-start.10 = (bf16[1,4608,128]{2,1,0:T(8,128)(2,1)S(1)}, bf16[1,4608,128]{2,1,0:T(8,128)(2,1)}, u32[]{:S(2)}) copy-start(bf16[1,4608,128]{2,1,0:T(8,128)(2,1)} %param.20) | copy-start | bytes 3538948
  106.4 2.9 %collective-permute-start = (bf16[512,128]{0,1:T(8,128)(2,1)S(1)}, bf16[512,128]{0,1:T(8,128)(2,1)S(1)}, u32[]{:S(2)}, u32[]{:S(2)}) collective-permute-start(bf16[512,128]{0,1:T(8,128)(2,1)S(1)} %fusion.21), channel_id=1, source_target_pairs={{0,1},{1,0},{2,3},{3,2},{4,5},{5,4},{6,7},{7,6},{8,9},{9,8},{10,11... | collective-permute-start | bytes 393224 | tf_op jit(solution)/shard_map/ppermute | solution.py:27
  113.6 1.3 copy-start.4
  120.1 6.6 %copy-start.7 = (f32[1,4608]{1,0:T(1,128)S(1)}, f32[1,4608]{1,0:T(1,128)}, u32[]{:S(2)}) copy-start(f32[1,4608]{1,0:T(1,128)} %param.23) | copy-start | bytes 55300
  120.1 39.7 %all-to-all-start.1 = ((bf16[32,1,9217]{2,1,0:T(2,128)(2,1)}), bf16[32,1,9217]{2,1,0:T(2,128)(2,1)S(1)}, u32[]{:S(2)}, u32[]{:S(2)}) async-start(bf16[32,1,9217]{2,1,0:T(2,128)(2,1)} %copy.22), calls=%async_computation.1 | async-start | bytes 2392064 | tf_op jit(solution)/shard_map/all_to_all | solution.py:13
  159.8 0.8 copy-start.2
  165.4 50.1 %copy-start.5 = (f32[4608]{0:T(1024)S(1)}, f32[4608]{0:T(1024)}, u32[]{:S(2)}) copy-start(f32[4608]{0:T(1024)} %reduce.2) | copy-start | bytes 55300
Sparse Core Ops, SparseCore 0:
  36.5 63.6 all-gather.2
  113.8 100.6 reduce-scatter.1
where the time goes:
time: 225 us; the launch traced here: 224 us
  waiting for transfers between devices  156 us (69%)
  local copies, waits for them, and re-layouts  15.7 us (7%)
  between operations  15.6 us (7%)
  other arithmetic  15.2 us (7%)
  starting transfers between devices  13.3 us (6%)
  matrix products  8 us (4%)
    all_gather x1, waiting for transfers between devices, on_device(): block_rows = lax.all_gather(checked, 'dp', axis=0, tiled=True)  61.9 us
    reduce_scatter x1, waiting for transfers between devices, on_device(): lax.psum_scatter(jnp.dot(attended, w_output, preferred_element_type=jnp.f...  47.4 us
    all_to_all x1, waiting for transfers between devices, sent_together(): lax.all_to_all(both, axis, split_axis=split_dim, concat_axis=concat_dim,...  32.2 us
    all_to_all x1, waiting for transfers between devices, on_device(): lax.all_to_all(outgoing, 'section', split_axis=0, concat_axis=0, tiled=True)  14.8 us
    all_to_all x1, starting transfers between devices, sent_together(): lax.all_to_all(both, axis, split_axis=split_dim, concat_axis=concat_dim,...  6.54 us
    all_to_all x1, starting transfers between devices, on_device(): lax.all_to_all(outgoing, 'section', split_axis=0, concat_axis=0, tiled=True)  6.18 us
    reduce_sum x2, other arithmetic, rms_norm(): meansq = jnp.mean(values * values, axis=-1, keepdims=True)  4.54 us
  transfers between devices with their start and end apart: 5, of which 4 were waited for; matrix products, arithmetic and copies ran while one was open for 7% of the time, Pallas kernels for 0%

commit v1 on v0

--- a/solution.py
+++ b/solution.py
@@ -4,6 +4,13 @@
 from jax.sharding import PartitionSpec as P
 
 D = 4608
+
+
+def all_by_exchange(shard, mesh_axis, d):
+    devices = lax.axis_size(mesh_axis)
+    shards = jnp.stack([shard for _ in range(devices)])
+    shards = lax.all_to_all(shards, mesh_axis, split_axis=0, concat_axis=0)
+    return jnp.concatenate(shards, axis=d)
 
 
 def sent_together(arrays, axis, split_dim, concat_dim, along):
@@ -110,7 +117,7 @@
     w_query = query_weight[0]
     w_keyval = keyval_weight[0]
     gain_pre = pre_gain[0]
-    block_rows = lax.all_gather(checked, "dp", axis=0, tiled=True)
+    block_rows = all_by_exchange(checked, "dp", 0)
     row_count = block_rows.shape[0]
     positions = jnp.arange(row_count, dtype=jnp.int32)
     normed = rms_norm(block_rows.astype(jnp.float32), gain_pre).astype(jnp.bfloat16)

time: 225 us -> 285 us (1.27)
  waiting for transfers between devices: 156 us -> 189 us
  starting transfers between devices: 13.3 us -> 36 us
  other arithmetic: 15.2 us -> 19 us
    all_to_all x0 -> x1, waiting for transfers between devices: none -> 83.5 us  [all_by_exchange(): shards = lax.all_to_all(shards, mesh_axis, split_axis=0, concat_axis=0)]
    all_gather x1 -> x0, waiting for transfers between devices: 61.9 us -> none  [on_device(): block_rows = lax.all_gather(checked, 'dp', axis=0, tiled=True)]
    reduce_scatter x1, waiting for transfers between devices: 47.4 us -> 63.9 us  [on_device(): lax.psum_scatter(jnp.dot(attended, w_output, preferred_element_type=jnp.f...]
    all_to_all x1, starting transfers between devices: 6.54 us -> 18.6 us  [sent_together(): lax.all_to_all(both, axis, split_axis=split_dim, concat_axis=concat_dim,...]
    all_to_all x0 -> x1, starting transfers between devices: none -> 10.8 us  [all_by_exchange(): shards = lax.all_to_all(shards, mesh_axis, split_axis=0, concat_axis=0)]
    all_to_all x1, waiting for transfers between devices: 32.2 us -> 26.3 us  [sent_together(): lax.all_to_all(both, axis, split_axis=split_dim, concat_axis=concat_dim,...]
    convert_element_type x0 -> x1, other arithmetic: none -> 3.98 us  [on_device(): rms_norm(block_rows.astype(jnp.float32), gain_pre).astype(jnp.bfloat16)]
  transfers between devices with their start and end apart: 5 -> 5, of which waited for: 4 -> 4; matrix products, arithmetic and copies ran while one was open for 7% -> 5% of each run, Pallas kernels for 0% -> 0%
where the time goes in v1:
time: 285 us; the launch traced here: 284 us
  waiting for transfers between devices  189 us (66%)
  starting transfers between devices  36 us (13%)
  other arithmetic  19 us (7%)
  local copies, waits for them, and re-layouts  17.5 us (6%)
  between operations  15.6 us (5%)
  matrix products  7.71 us (3%)
    all_to_all x1, waiting for transfers between devices, all_by_exchange(): shards = lax.all_to_all(shards, mesh_axis, split_axis=0, concat_axis=0)  83.5 us
    reduce_scatter x1, waiting for transfers between devices, on_device(): lax.psum_scatter(jnp.dot(attended, w_output, preferred_element_type=jnp.f...  63.9 us
    all_to_all x1, waiting for transfers between devices, sent_together(): lax.all_to_all(both, axis, split_axis=split_dim, concat_axis=concat_dim,...  26.3 us
    all_to_all x1, starting transfers between devices, sent_together(): lax.all_to_all(both, axis, split_axis=split_dim, concat_axis=concat_dim,...  18.6 us
    all_to_all x1, waiting for transfers between devices, on_device(): lax.all_to_all(outgoing, 'section', split_axis=0, concat_axis=0, tiled=True)  14.8 us
    all_to_all x1, starting transfers between devices, all_by_exchange(): shards = lax.all_to_all(shards, mesh_axis, split_axis=0, concat_axis=0)  10.8 us
    all_to_all x1, starting transfers between devices, on_device(): lax.all_to_all(outgoing, 'section', split_axis=0, concat_axis=0, tiled=True)  6.18 us
  transfers between devices with their start and end apart: 5, of which 4 were waited for; matrix products, arithmetic and copies ran while one was open for 5% of the time, Pallas kernels for 0%

profile of v1, /device:TPU:2, one launch (start us, length us, event | category | flops | bytes accessed | tf_op | source)
XLA Modules:
  0.0 284.3 jit_solution(4654186658810611886)
XLA Ops:
  7.2 0.8 reshape.138
  8.1 0.7 sort.34
  9.5 1.9 gather_fusion.2
  11.4 1.2 broadcast_select_fusion.1
  12.6 6.2 %all-to-all-start = ((bf16[8,16,4608]{2,1,0:T(8,128)(2,1)}), bf16[8,16,4608]{2,1,0:T(8,128)(2,1)S(1)}, u32[]{:S(2)}, u32[]{:S(2)}) async-start(bf16[8,16,4608]{2,1,0:T(8,128)(2,1)} %broadcast_select_fusion.1), calls=%async_computation | async-start | bytes 2359296 | tf_op jit(solution)/shard_map/all_to_all | solution.py:90
  19.0 14.8 %all-to-all-done = bf16[8,16,4608]{2,1,0:T(8,128)(2,1)S(1)} async-done(((bf16[8,16,4608]{2,1,0:T(8,128)(2,1)}), bf16[8,16,4608]{2,1,0:T(8,128)(2,1)S(1)}, u32[]{:S(2)}, u32[]{:S(2)}) %all-to-all-start) | async-done | bytes 1179680 | tf_op jit(solution)/shard_map/all_to_all | solution.py:90
  34.6 1.0 copy-done.2
  35.6 2.7 stack.3
  38.3 10.8 %all-to-all-start.2 = ((bf16[32,16,4608]{2,1,0:T(8,128)(2,1)}), bf16[32,16,4608]{2,1,0:T(8,128)(2,1)}, u32[]{:S(2)}, u32[]{:S(2)}) async-start(bf16[32,16,4608]{2,1,0:T(8,128)(2,1)} %stack.3), calls=%async_computation.2 | async-start | bytes 9437184 | tf_op jit(solution)/shard_map/all_to_all | solution.py:12
  49.5 0.8 sort.35
  50.3 0.7 gather_fusion.1
  51.1 83.5 %all-to-all-done.2 = bf16[32,16,4608]{2,1,0:T(8,128)(2,1)} async-done(((bf16[32,16,4608]{2,1,0:T(8,128)(2,1)}), bf16[32,16,4608]{2,1,0:T(8,128)(2,1)}, u32[]{:S(2)}, u32[]{:S(2)}) %all-to-all-start.2) | async-done | bytes 4718624 | tf_op jit(solution)/shard_map/all_to_all | solution.py:12
  134.5 3.3 %fusion = f32[32,16]{1,0:T(8,128)S(1)} fusion(bf16[32,16,4608]{2,1,0:T(8,128)(2,1)} %all-to-all-done.2), kind=kLoop, calls=%fused_computation.8 | loop fusion | flops 7077376 | bytes 4720640 | tf_op jit(solution)/shard_map/reduce_sum | solution.py:38
  137.9 4.0 %fusion.2 = bf16[32,16,4608]{2,1,0:T(8,128)(2,1)S(1)} fusion(bf16[32,16,4608]{2,1,0:T(8,128)(2,1)} %all-to-all-done.2, f32[4608]{0:T(1024)S(1)} %reduce.2, f32[32,16]{1,0:T(8,128)S(1)} %add_rsqrt_fusion), kind=kLoop, calls=%fused_computation.10 | loop fusion | flops 9437184 | bytes 9457664 | tf_op jit(solution)/shard_map/convert_element_type | solution.py:123
  141.9 1.7 fusion.8
  144.5 1.7 fusion.10
  147.2 3.9 %convolution_convert_fusion = bf16[512,4608]{1,0:T(8,128)(2,1)} fusion(bf16[1,128,4608]{2,1,0:T(8,128)(2,1)S(1)} %copy-done, bf16[512,512]{0,1:T(8,128)(2,1)S(1)} %get-tuple-element.28, f32[512]{0:T(512)S(1)} %get-tuple-element.27, bf16[512,128]{0,1:T(8,128)(2,1)S(1)} %collective-permute-done, bf16[512,128]{0,1:T(8,128)(2,1)S(1)} %fusion.19, pred[]{:T(512)S(6)} %eq.57), kind=kOutput, calls=%fused_computation.11 | convolution fusion | flops 673644544 | bytes 6686721 | tf_op jit(solution)/shard_map/dot_general | solution.py:152
  151.2 1.2 copy-done.5
  152.4 1.8 gather_fusion.4
  154.2 0.6 select_convert_fusion
  155.6 2.0 copy.22
  157.5 18.6 %all-to-all-start.1 = ((bf16[32,1,9217]{2,1,0:T(2,128)(2,1)}), bf16[32,1,9217]{2,1,0:T(2,128)(2,1)S(1)}, u32[]{:S(2)}, u32[]{:S(2)}) async-start(bf16[32,1,9217]{2,1,0:T(2,128)(2,1)} %copy.22), calls=%async_computation.1 | async-start | bytes 2392064 | tf_op jit(solution)/shard_map/all_to_all | solution.py:20
  176.2 0.7 reduce.3
  177.1 26.3 %all-to-all-done.1 = bf16[32,1,9217]{2,1,0:T(2,128)(2,1)S(1)} async-done(((bf16[32,1,9217]{2,1,0:T(2,128)(2,1)}), bf16[32,1,9217]{2,1,0:T(2,128)(2,1)S(1)}, u32[]{:S(2)}, u32[]{:S(2)}) %all-to-all-start.1) | async-done | bytes 589920 | tf_op jit(solution)/shard_map/all_to_all | solution.py:20
  203.5 0.8 copy-done.1
  204.4 1.0 reshape.145
  205.4 1.8 gather_fusion.5
  207.2 1.3 convert_reduce_fusion
  209.1 1.6 select_multiply_fusion
  210.7 63.9 %reduce-scatter.2.cloned.1.call-done = bf16[16,4608]{1,0:T(8,128)(2,1)} async-done(((bf16[512,4608]{1,0:T(8,128)(2,1)}), bf16[16,4608]{1,0:T(8,128)(2,1)}) %reduce-scatter.2.cloned.1.call-update) | async-done | bytes 147472 | tf_op jit(solution)/shard_map/reduce_scatter | solution.py:151
  274.6 1.1 fusion.15
  275.7 1.8 fusion.28
  (67 shorter events, 4.5 us)
Async XLA Ops:
  7.2 140.0 %copy-start = (bf16[1,128,4608]{2,1,0:T(8,128)(2,1)S(1)}, bf16[1,128,4608]{2,1,0:T(8,128)(2,1)}, u32[]{:S(2)}) copy-start(bf16[1,128,4608]{2,1,0:T(8,128)(2,1)} %param.22) | copy-start | bytes 3538948
  12.6 21.2 %all-to-all-start = ((bf16[8,16,4608]{2,1,0:T(8,128)(2,1)}), bf16[8,16,4608]{2,1,0:T(8,128)(2,1)S(1)}, u32[]{:S(2)}, u32[]{:S(2)}) async-start(bf16[8,16,4608]{2,1,0:T(8,128)(2,1)} %broadcast_select_fusion.1), calls=%async_computation | async-start | bytes 2359296 | tf_op jit(solution)/shard_map/all_to_all | solution.py:90
  34.6 1.0 copy-start.2
  38.3 10.9 %copy-start.9 = (s32[1024]{0:T(1024)S(1)}, s32[1024]{0:T(1024)}, u32[]{:S(2)}) copy-start(s32[1024]{0:T(1024)} %param.17) | copy-start | bytes 12292
  38.3 11.1 %copy-start.7 = (f32[1,4608]{1,0:T(1,128)S(1)}, f32[1,4608]{1,0:T(1,128)}, u32[]{:S(2)}) copy-start(f32[1,4608]{1,0:T(1,128)} %param.19) | copy-start | bytes 55300
  38.3 96.2 %all-to-all-start.2 = ((bf16[32,16,4608]{2,1,0:T(8,128)(2,1)}), bf16[32,16,4608]{2,1,0:T(8,128)(2,1)}, u32[]{:S(2)}, u32[]{:S(2)}) async-start(bf16[32,16,4608]{2,1,0:T(8,128)(2,1)} %stack.3), calls=%async_computation.2 | async-start | bytes 9437184 | tf_op jit(solution)/shard_map/all_to_all | solution.py:12
  49.2 225.4 %reduce-scatter.2.cloned.1.call-start = ((), (), s32[]{:S(2)}) async-start(), calls=%async_computation.4 | async-start | bytes 4866048 | tf_op jit(solution)/shard_map/reduce_scatter | solution.py:151
  137.9 4.0 %copy-start.3 = (bf16[1,4608,128]{2,1,0:T(8,128)(2,1)S(1)}, bf16[1,4608,128]{2,1,0:T(8,128)(2,1)}, u32[]{:S(2)}) copy-start(bf16[1,4608,128]{2,1,0:T(8,128)(2,1)} %param.21) | copy-start | bytes 3538948
  141.9 2.6 copy-start.4
  144.2 2.6 collective-permute-start
  151.1 1.3 copy-start.5
  157.5 18.7 %copy-start.8 = (f32[1,4608]{1,0:T(1,128)S(1)}, f32[1,4608]{1,0:T(1,128)}, u32[]{:S(2)}) copy-start(f32[1,4608]{1,0:T(1,128)} %param.23) | copy-start | bytes 55300
  157.5 45.9 %all-to-all-start.1 = ((bf16[32,1,9217]{2,1,0:T(2,128)(2,1)}), bf16[32,1,9217]{2,1,0:T(2,128)(2,1)S(1)}, u32[]{:S(2)}, u32[]{:S(2)}) async-start(bf16[32,1,9217]{2,1,0:T(2,128)(2,1)} %copy.22), calls=%async_computation.1 | async-start | bytes 2392064 | tf_op jit(solution)/shard_map/all_to_all | solution.py:20
  203.5 0.8 copy-start.1
  209.1 66.6 %copy-start.6 = (f32[4608]{0:T(1024)S(1)}, f32[4608]{0:T(1024)}, u32[]{:S(2)}) copy-start(f32[4608]{0:T(1024)} %reduce.3) | copy-start | bytes 55300
Sparse Core Ops, SparseCore 0:
  151.2 123.3 reduce-scatter.1
